TPU v7x, 32 devices: a whole 2x2x4 slice. The times are simulated.
32 devices in a mesh: section: 16 (over z, y, core), tensor: 2 (over x).
Axes of the slice: x: 2, y: 2, z: 4, core: 2. Of those that a mesh axis runs over, the one named last changes fastest.
Arguments:
- saved: bfloat16 [16, 16, 64, 8192], P('section', None, 'tensor'), may hold values from -6 to 6
- offsets: int32 [16, 16], P('section'), may hold values from 0 to 15, as said below
Outputs:
- restored: float32 [16, 16, 64, 8192], P('section', None, None, 'tensor')
- block_sums: float32 [16, 16, 8192], P('section', None, 'tensor')
Inputs may be any that keep to these rules, and one draw needn't show every extreme that they name: Each row of offsets is a permutation of 0 to 15.
All inputs are finite; a program needn't handle non-finite values.
Results may differ from a plain program's by a relative error of at most 0.0003.
Values may be sent and summed in bfloat16 or wider, within the bound.
A program may use at most 128 MiB of HBM per device.

v0:
```python
import jax
import jax.numpy as jnp
from jax import lax
from jax.sharding import PartitionSpec as P


def invert(table, count):
    return jnp.zeros((count,), jnp.int32).at[table].set(jnp.arange(count, dtype=jnp.int32))


def body(saved, offsets):
    count = lax.axis_size("section")
    mine = lax.axis_index("section")
    table = offsets[0]
    blocks = saved[0]
    order = invert((mine + table) % count, count)
    outgoing = jnp.take(blocks, order, axis=0)
    split_cols = lax.all_to_all(outgoing, "tensor", split_axis=2, concat_axis=1, tiled=True)
    arrived = lax.all_to_all(split_cols, "section", split_axis=0, concat_axis=0, tiled=True)
    restored = arrived.astype(jnp.float32)
    block_sums = jnp.sum(restored, axis=1)
    return (restored[None], block_sums[None])


def solution(mesh):
    return jax.shard_map(
        body,
        mesh=mesh,
        in_specs=(P("section", None, "tensor", None), P("section", None)),
        out_specs=(P("section", None, None, "tensor"), P("section", None, "tensor")),
        check_vma=False,
    )
```

profile of v0, /device:TPU:1, one launch (start us, length us, event | category | flops | bytes accessed | tf_op | source)
XLA Modules:
  0.0 462.9 jit_solution(6065663858853515315)
XLA Ops:
  0.6 0.7 fusion.1
  1.3 0.6 scatter_custom_fusion
  2.0 8.3 %gather_fusion = bf16[16,32,8192]{2,1,0:T(8,128)(2,1)} fusion(bf16[16,32,8192]{2,1,0:T(8,128)(2,1)} %bitcast.18, s32[1024]{0:T(1024)S(1)} %pad_clamp_fusion), kind=kCustom, calls=%fused_computation | custom fusion | bytes 16777280 | tf_op jit(solution)/shard_map/jit(_take)/gather | solution.py:17
  10.3 7.6 %broadcast_select_fusion = bf16[16,32,8192]{2,1,0:T(8,128)(2,1)} fusion(bf16[16,32,8192]{2,1,0:T(8,128)(2,1)} %gather_fusion, pred[16]{0:T(512)(128)(4,1)S(1)} %compare_and_fusion), kind=kLoop, calls=%fused_computation.4 | loop fusion | flops 4194304 | bytes 16777232 | tf_op jit(solution)/shard_map/jit(_take)/select_n | solution.py:17
  17.9 34.7 %copy.6 = bf16[16,32,8192]{1,0,2:T(8,128)(2,1)} copy(bf16[16,32,8192]{2,1,0:T(8,128)(2,1)} %broadcast_select_fusion) | data formatting | bytes 16777216 | tf_op jit(solution)/shard_map/jit(_take)/select_n | solution.py:17
  52.6 27.6 %reshape.82 = bf16[2,2,1048576]{2,1,0:T(2,128)(2,1)} reshape(bf16[8192,16,32]{2,1,0:T(8,128)(2,1)} %bitcast.15) | data formatting | bytes 16777216
  80.2 103.8 %all_to_all.23 = bf16[2,2,1048576]{2,1,0:T(2,128)(2,1)} all-to-all(bf16[2,2,1048576]{2,1,0:T(2,128)(2,1)} %reshape.82), channel_id=1, replica_groups=mesh['section'=16,'tensor'=2] {'tensor'}, dimensions={0} | all-to-all | bytes 16777216 | tf_op jit(solution)/shard_map/all_to_all | solution.py:18
  184.0 38.0 %reshape.83 = bf16[8192,16,32]{2,1,0:T(8,128)(2,1)} reshape(bf16[2,2,1048576]{2,1,0:T(2,128)(2,1)} %all_to_all.23) | data formatting | bytes 16777216
  222.0 33.7 %copy.7 = bf16[16,2,32,4096]{3,2,1,0:T(8,128)(2,1)} copy(bf16[16,2,32,4096]{2,0,3,1:T(8,128)(2,1)} %bitcast.16) | data formatting | bytes 16777216 | tf_op jit(solution)/shard_map/all_to_all | solution.py:18
  255.8 189.7 %all_to_all.24 = bf16[16,64,4096]{2,1,0:T(8,128)(2,1)S(1)} all-to-all(bf16[16,64,4096]{2,1,0:T(8,128)(2,1)} %bitcast.17), channel_id=1, replica_groups=mesh['section'=16,'tensor'=2] {'section'}, dimensions={0} | all-to-all | bytes 16777216 | tf_op jit(solution)/shard_map/all_to_all | solution.py:19
  445.4 0.0 copy-start
  445.5 3.2 copy-done
  448.7 2.4 convert_reduce_fusion
  451.1 11.8 %convert_bitcast_fusion = f32[1,16,64,4096]{3,2,1,0:T(8,128)} fusion(bf16[16,64,4096]{2,1,0:T(8,128)(2,1)} %copy-done), kind=kLoop, calls=%fused_computation.3 | loop fusion | flops 4194304 | bytes 25165824 | tf_op jit(solution)/shard_map/broadcast_in_dim | solution.py:22
  (4 shorter events, 0.0 us)
Async XLA Ops:
  445.4 3.2 copy-start
where the time goes:
time: 465 us; the launch traced here: 463 us
  blocking collectives  294 us (63%)
  local copies, waits for them, and re-layouts  146 us (31%)
  other arithmetic  22.6 us (5%)
    all_to_all x1, blocking collectives, body(): lax.all_to_all(split_cols, 'section', split_axis=0, concat_axis=0, tiled=...  190 us
    all_to_all x1, blocking collectives, body(): lax.all_to_all(outgoing, 'tensor', split_axis=2, concat_axis=1, tiled=True)  104 us
    unnamed x4, local copies, waits for them, and re-layouts  68.8 us
    select_n x1, local copies, waits for them, and re-layouts, body(): outgoing = jnp.take(blocks, order, axis=0)  34.7 us
    all_to_all x1, local copies, waits for them, and re-layouts, body(): lax.all_to_all(outgoing, 'tensor', split_axis=2, concat_axis=1, tiled=True)  33.7 us
    broadcast_in_dim x1, other arithmetic, body(): return (restored[None], block_sums[None])  11.8 us

commit v1 on v0

--- a/solution.py
+++ b/solution.py
@@ -15,7 +15,9 @@
     blocks = saved[0]
     order = invert((mine + table) % count, count)
     outgoing = jnp.take(blocks, order, axis=0)
-    split_cols = lax.all_to_all(outgoing, "tensor", split_axis=2, concat_axis=1, tiled=True)
+    cells = jnp.split(outgoing, lax.axis_size("tensor"), axis=2)
+    got = lax.all_to_all(jnp.stack(cells), "tensor", 0, 0)
+    split_cols = jnp.concatenate(got, axis=1)
     arrived = lax.all_to_all(split_cols, "section", split_axis=0, concat_axis=0, tiled=True)
     restored = arrived.astype(jnp.float32)
     block_sums = jnp.sum(restored, axis=1)

time: 465 us -> 349 us (0.75)
  local copies, waits for them, and re-layouts: 146 us -> 25.2 us
  other arithmetic: 22.6 us -> 28.9 us
    unnamed x4 -> x2, local copies, waits for them, and re-layouts: 68.8 us -> 3.22 us
    select_n x1 -> x0, local copies, waits for them, and re-layouts: 34.7 us -> none  [body(): outgoing = jnp.take(blocks, order, axis=0)]
    all_to_all x1 -> x0, local copies, waits for them, and re-layouts: 33.7 us -> none  [body(): lax.all_to_all(outgoing, 'tensor', split_axis=2, concat_axis=1, tiled=True)]
    reshape x0 -> x1, local copies, waits for them, and re-layouts: none -> 7.89 us  [body(): split_cols = jnp.concatenate(got, axis=1)]
    another operation x0 -> x1, other arithmetic: none -> 6.35 us  [body(): got = lax.all_to_all(jnp.stack(cells), 'tensor', 0, 0)]
    another operation x0 -> x1, local copies, waits for them, and re-layouts: none -> 5.13 us  [body(): got = lax.all_to_all(jnp.stack(cells), 'tensor', 0, 0)]
where the time goes in v1:
time: 349 us; the launch traced here: 348 us
  blocking collectives  293 us (84%)
  other arithmetic  28.9 us (8%)
  local copies, waits for them, and re-layouts  25.2 us (7%)
    all_to_all x1, blocking collectives, body(): lax.all_to_all(split_cols, 'section', split_axis=0, concat_axis=0, tiled=...  190 us
    all_to_all x1, blocking collectives, body(): got = lax.all_to_all(jnp.stack(cells), 'tensor', 0, 0)  104 us
    broadcast_in_dim x1, other arithmetic, body(): return (restored[None], block_sums[None])  11.8 us
    gather x1, local copies, waits for them, and re-layouts, body(): outgoing = jnp.take(blocks, order, axis=0)  8.32 us
    reshape x1, local copies, waits for them, and re-layouts, body(): split_cols = jnp.concatenate(got, axis=1)  7.89 us
    select_n x2, other arithmetic, body(): outgoing = jnp.take(blocks, order, axis=0)  7.65 us

profile of v1, /device:TPU:1, one launch (start us, length us, event | category | flops | bytes accessed | tf_op | source)
XLA Modules:
  0.0 348.3 jit_solution(569677759240871215)
XLA Ops:
  0.6 0.7 fusion.1
  1.3 0.6 scatter_custom_fusion
  2.0 8.3 %gather_fusion = bf16[16,32,8192]{2,1,0:T(8,128)(2,1)} fusion(bf16[16,32,8192]{2,1,0:T(8,128)(2,1)} %bitcast.17, s32[1024]{0:T(1024)S(1)} %pad_clamp_fusion), kind=kCustom, calls=%fused_computation | custom fusion | bytes 16777280 | tf_op jit(solution)/shard_map/jit(_take)/gather | solution.py:17
  10.3 7.6 %broadcast_select_fusion = bf16[16,32,8192]{2,1,0:T(8,128)(2,1)} fusion(bf16[16,32,8192]{2,1,0:T(8,128)(2,1)} %gather_fusion, pred[16]{0:T(512)(128)(4,1)S(1)} %compare_and_fusion), kind=kLoop, calls=%fused_computation.5 | loop fusion | flops 4194304 | bytes 16777232 | tf_op jit(solution)/shard_map/jit(_take)/select_n | solution.py:17
  17.9 5.1 %slice_bitcast_fusion.1 = (bf16[1,16,32,4096]{3,2,1,0:T(8,128)(2,1)S(1)}, bf16[1,16,32,4096]{3,2,1,0:T(8,128)(2,1)}) fusion(bf16[16,32,8192]{2,1,0:T(8,128)(2,1)} %broadcast_select_fusion), kind=kLoop, calls=%fused_computation.7 | loop fusion | bytes 16777216 | tf_op jit(solution)/shard_map/stack | solution.py:19
  23.1 6.3 %pad_maximum_fusion = bf16[2,16,32,4096]{3,2,1,0:T(8,128)(2,1)} fusion(bf16[1,16,32,4096]{3,2,1,0:T(8,128)(2,1)} %get-tuple-element.3, bf16[1,16,32,4096]{3,2,1,0:T(8,128)(2,1)S(1)} %get-tuple-element.2), kind=kLoop, calls=%fused_computation.4 | loop fusion | flops 4194304 | bytes 16777216 | tf_op jit(solution)/shard_map/stack | solution.py:19
  29.4 103.6 %all_to_all.10 = bf16[2,16,32,4096]{3,2,1,0:T(8,128)(2,1)} all-to-all(bf16[2,16,32,4096]{3,2,1,0:T(8,128)(2,1)} %pad_maximum_fusion), channel_id=1, replica_groups=mesh['section'=16,'tensor'=2] {'tensor'}, dimensions={0} | all-to-all | bytes 16777216 | tf_op jit(solution)/shard_map/all_to_all | solution.py:19
  133.0 7.9 %copy.4 = bf16[16,2,32,4096]{3,2,1,0:T(8,128)(2,1)} copy(bf16[16,2,32,4096]{3,2,0,1:T(8,128)(2,1)} %bitcast.15) | data formatting | bytes 16777216 | tf_op jit(solution)/shard_map/reshape | solution.py:20
  140.9 189.9 %all_to_all.11 = bf16[16,64,4096]{2,1,0:T(8,128)(2,1)S(1)} all-to-all(bf16[16,64,4096]{2,1,0:T(8,128)(2,1)} %bitcast.16), channel_id=1, replica_groups=mesh['section'=16,'tensor'=2] {'section'}, dimensions={0} | all-to-all | bytes 16777216 | tf_op jit(solution)/shard_map/all_to_all | solution.py:21
  330.8 0.0 copy-start
  330.8 3.2 copy-done
  334.0 2.4 convert_reduce_fusion
  336.5 11.8 %convert_bitcast_fusion = f32[1,16,64,4096]{3,2,1,0:T(8,128)} fusion(bf16[16,64,4096]{2,1,0:T(8,128)(2,1)} %copy-done), kind=kLoop, calls=%fused_computation.3 | loop fusion | flops 4194304 | bytes 25165824 | tf_op jit(solution)/shard_map/broadcast_in_dim | solution.py:24
  (4 shorter events, 0.0 us)
Async XLA Ops:
  330.8 3.2 copy-start
